TPU v7x, 16 devices: a whole 2x2x2 slice. The times are simulated.
16 devices in a mesh: data: 16 (over z, y, x, core).
Axes of the slice: x: 2, y: 2, z: 2, core: 2. Of those that a mesh axis runs over, the one named last changes fastest.
Arguments:
- w_in: float32 [2304, 384], replicated
- w_up: float32 [16, 384, 1536], replicated
- w_down: float32 [16, 1536, 384], replicated
- mom_in: float32 [2304, 384], replicated
- mom_up: float32 [16, 384, 1536], replicated
- mom_down: float32 [16, 1536, 384], replicated
- x_now: bfloat16 [8192, 2304], P('data')
- y_now: bfloat16 [8192, 384], P('data')
- x_next: bfloat16 [8192, 2304], P('data')
- y_next: bfloat16 [8192, 384], P('data')
Outputs:
- output 1: float32 [2304, 384], replicated
- output 2: float32 [16, 384, 1536], replicated
- output 3: float32 [16, 1536, 384], replicated
- output 4: float32 [2304, 384], replicated
- output 5: float32 [16, 384, 1536], replicated
- output 6: float32 [16, 1536, 384], replicated
- output 7: float32 [8192], P('data')
- output 8: float32 [8192, 384], P('data')
All inputs are finite; a program needn't handle non-finite values.
Results may differ from a plain program's by a relative error of at most 0.010136.
Values are sent between devices in bfloat16 or wider.
A program may use at most 1.25 GiB of HBM per device.

v0:
```python
import functools

import jax
import jax.numpy as jnp
from jax import lax
from jax.experimental import pallas as pl
from jax.experimental.pallas import tpu as pltpu
from jax.sharding import PartitionSpec as P


MOMENTUM = 0.9
BF = jnp.bfloat16
F32 = jnp.float32
MESH = pl.DeviceIdType.MESH
ANY = pl.BlockSpec(memory_space=pl.ANY)
VM = pl.BlockSpec(memory_space=pltpu.VMEM)
L, D, FF, E, ROWS = 16, 384, 1536, 2304, 512
NC = 3
GROUPS = ((0, 1), (1, 3), (4, 5), (9, 7))
N_OUT = NC * (2 * len(GROUPS) + 6)
KAPPA = 0.7978845608028654


def dot(a, b, ca, cb):
    return lax.dot_general(a, b, (((ca,), (cb,)), ((), ())), preferred_element_type=F32)


def gelu_parts(u):
    u2 = u * u
    t = jnp.tanh(u * (KAPPA + (KAPPA * 0.044715) * u2))
    cdf = 0.5 + 0.5 * t
    return u2, t, cdf


def gelu_low(u):
    _, _, cdf = gelu_parts(u)
    return (u * cdf).astype(BF)


def gelu_both(u):
    u2, t, cdf = gelu_parts(u)
    grad = cdf + (0.5 * u) * (1.0 - t * t) * (KAPPA + (3.0 * KAPPA * 0.044715) * u2)
    return (u * cdf).astype(BF), grad


def position():
    me = lax.axis_index("data")
    bits = [(me // (2 << d)) % 2 for d in range(3)]
    cores = me % 2
    partner = [me + (2 << d) * (1 - 2 * bits[d]) for d in range(3)]
    return cores, me + 1 - 2 * cores, bits, partner


class Unit:
    def __init__(self, grad, recv, hold, whole, size, send, take, pos):
        self.grad, self.recv, self.hold, self.whole = grad, recv, hold, whole
        self.size, self.send, self.take = size, send, take
        self.core, self.mate, bits, partner = pos
        self.dims = [[(k + s) % 3 for s in range(3)] for k in range(NC)]
        self.bit = [[bits[d] for d in self.dims[k]] for k in range(NC)]
        self.to = [[partner[d] for d in self.dims[k]] for k in range(NC)]

    def rows(self, start, count):
        return pl.ds(pl.multiple_of(start, 16), count)

    def low(self, k, s):
        at = 0
        for step in range(s):
            at = at + self.bit[k][step] * (self.size >> (step + 1))
        return at

    def halving(self, k, s):
        if s == 0:
            return self.copy(self.grad(k, 1 - self.core, None), self.recv(0, k), self.mate, s, k)
        count = self.size >> s
        away = self.low(k, s - 1) + (1 - self.bit[k][s - 1]) * count
        return self.copy(self.grad(k, self.core, self.rows(away, count)), self.recv(s, k), self.to[k][s - 1], s, k)

    def doubling(self, k, s):
        part = self.rows(self.low(k, s) - self.low(k, 1), self.size >> s)
        return self.copy(self.hold(k, part), self.hold(k, part), self.to[k][s - 1], 7 - s, k)

    def across(self, k, s):
        own, mine, far, both = self.whole
        src, dst, dev = {6: (own, mine, self.mate), 7: (own, far, self.to[k][0]), 8: (far, both, self.mate)}[s]
        return self.copy(src(k), dst(k), dev, s, k)

    def step(self, s, k):
        if s < 4:
            return self.halving(k, s)
        return self.doubling(k, 7 - s) if s < 6 else self.across(k, s)

    def copy(self, src, dst, dev, s, k):
        return pltpu.make_async_remote_copy(
            src_ref=src, dst_ref=dst, send_sem=self.send(s, k), recv_sem=self.take(s, k),
            device_id=(dev,), device_id_type=MESH)

    def start(self, s):
        for k in range(NC):
            self.step(s, k).start()

    def wait(self, s):
        for k in range(NC):
            self.step(s, k).wait()

    def follow(self, s, *nexts):
        for k in range(NC):
            self.step(s, k).wait()
            for n in nexts:
                self.step(n, k).start()

    def reduce(self, s):
        for k in range(NC):
            self.step(s, k).wait()
            count = self.size >> s
            mine = self.grad(k, self.core, self.rows(self.low(k, s), count))
            total = mine[...] + self.recv(s, k)[...]
            if s < 3:
                mine[...] = total
                self.halving(k, s + 1).start()
            else:
                self.hold(k, self.rows(self.low(k, 3) - self.low(k, 1), count))[...] = total
                self.doubling(k, 3).start()


def first_kernel(scale, *refs):
    w_in, w_up, w_down, x_hbm, y_hbm = refs[:5]
    n_out = N_OUT
    out = refs[5:5 + n_out]
    (st1, st2, acts, grads, gin, r0, r1, r2, r3, q0, q1, q2, q3, hold, mates, far, both, hin, min_, fin, bin_,
     xb, yb, state, low, send, take, send_in, take_in, ld1, ld2, ldx, ho, hx) = refs[5 + n_out:]
    pos = position()

    barrier = pltpu.get_barrier_semaphore()
    for dev in [pos[1]] + pos[3]:
        pl.semaphore_signal(barrier, inc=1, device_id=(dev,), device_id_type=MESH)
    pl.semaphore_wait(barrier, 4)

    def load1(l):
        return pltpu.make_async_copy(w_up.at[l], st1.at[l % 2], ld1.at[l % 2])

    def load2(l):
        return pltpu.make_async_copy(w_down.at[l], st2.at[l % 2], ld2.at[l % 2])

    load_x = pltpu.make_async_copy(x_hbm, xb, ldx.at[0])
    load_y = pltpu.make_async_copy(y_hbm, yb, ldx.at[1])
    load_a = pltpu.make_async_copy(w_in.at[pl.ds(0, 1536)], st2.at[0], ld2.at[0])
    load_b = pltpu.make_async_copy(w_in.at[pl.ds(1536, 768)], st2.at[1, pl.ds(0, 768)], ld2.at[1])
    load_x.start()
    load_a.start()
    load_b.start()
    load1(0).start()
    load1(1).start()
    load_y.start()
    load_x.wait()
    load_a.wait()
    state[...] = dot(xb[:, :1536], st2[0].astype(BF), 1, 0)
    load2(0).start()
    load_b.wait()
    state[...] += dot(xb[:, 1536:], st2[1, :768].astype(BF), 1, 0)
    load2(1).start()

    @pl.loop(0, L)
    def _(l):
        slot = l % 2
        p = state[...].astype(BF)
        acts[l] = p
        load1(l).wait()
        load2(l).wait()

        for j in range(3):
            cols = slice(j * 512, j * 512 + 512)
            a = gelu_low(dot(p, st1[slot, :, cols].astype(BF), 1, 0))
            state[...] += dot(a, st2[slot, cols, :].astype(BF), 1, 0)

        @pl.when(l + 2 < L)
        def _():
            load1(l + 2).start()
            load2(l + 2).start()

    load_y.wait()
    state[...] = (state[...] - yb[...].astype(F32)) * scale

    def job(i):
        par = i % 2

        def recv(s, k):
            return (r0, r1, r2, r3)[s].at[par, k]

        def grad(k, c, rows):
            ref = grads.at[i % 4, k, c]
            return ref if rows is None else ref.at[:, rows, :]

        whole = (lambda k: hold.at[i % 4, k], lambda k: mates.at[i % 3, k], lambda k: far.at[k], lambda k: both.at[k])
        return Unit(grad, recv, lambda k, rows: hold.at[i % 4, k, :, rows, :], whole, 256,
                    lambda s, k: send.at[s, par, k], lambda s, k: take.at[s, par, k], pos)

    def job_in():
        def grad(k, c, rows):
            ref = gin.at[k, c]
            return ref if rows is None else ref.at[rows, :]

        return Unit(grad, lambda s, k: (q0, q1, q2, q3)[s].at[k], lambda k, rows: hin.at[k, rows, :],
                    tuple((lambda k, ref=ref: ref.at[k]) for ref in (hin, min_, fin, bin_)), 384,
                    lambda s, k: send_in.at[s, k], lambda s, k: take_in.at[s, k], pos)

    def put(i, which, begin):
        l = L - 1 - i
        for g, (first, count) in enumerate(GROUPS):
            @pl.when((l >= first) & (l < first + count))
            def _():
                for k in range(NC):
                    c = pltpu.make_async_copy(hold.at[i % 4, k] if which == 0 else mates.at[i % 3, k],
                                              out[(g * 2 + which) * NC + k].at[l - first], ho.at[i % 2, which, k])
                    if begin:
                        c.start()
                    else:
                        c.wait()

    def during(i, lag, step):
        pl.when((i >= lag) & (i < L + lag))(step)

    def middle(i):
        during(i, 2, lambda: job(i - 2).reduce(1))
        pl.when(i == 18)(lambda: job_in().reduce(1))
        during(i, 1, lambda: job(i - 1).reduce(0))
        pl.when(i == 17)(lambda: job_in().reduce(0))

        @functools.partial(during, i, 6)
        def _():
            put(i - 6, 0, False)
            put(i - 6, 1, False)

        during(i, 3, lambda: job(i - 3).reduce(3))
        pl.when(i == 19)(lambda: job_in().reduce(3))

        @functools.partial(during, i, 5)
        def _():
            job(i - 5).follow(5, 6)
            put(i - 5, 0, True)

        pl.when(i == L + 4)(lambda: job(L - 1).start(7))
        during(i, 4, lambda: job(i - 4).follow(4, 5))

    def end(i):
        during(i, 2, lambda: job(i - 2).reduce(2))
        pl.when(i == 18)(lambda: job_in().reduce(2))
        pl.when(i == 19)(lambda: job_in().follow(4, 5))

        @functools.partial(during, i, 5)
        def _():
            job(i - 5).wait(6)
            put(i - 5, 1, True)

        during(i, 0, lambda: job(i).start(0))
        pl.when(i == L)(lambda: job_in().start(0))

    @pl.loop(0, L + 5)
    def _(i):
        @pl.when(i < L)
        def _():
            @pl.when(i >= 2)
            def _():
                load1(L - 1 - i).wait()
                load2(L - 1 - i).wait()

            low[...] = state[...].astype(BF)

        @pl.loop(0, 3)
        def _(k):
            @pl.when(k == 1)
            def _():
                middle(i)

            @pl.when(i < L)
            def _():
                slot = (L - 1 - i) % 2
                p = acts[L - 1 - i]
                cot = low[...]
                add = None
                for half in range(2):
                    at = pl.multiple_of(k * 512 + half * 256, 256)
                    cols = pl.ds(at, 256)
                    w1 = st1[slot, :, cols].astype(BF)
                    w2 = st2[slot, cols, :].astype(BF)
                    a, slope = gelu_both(dot(p, w1, 1, 0))
                    q = (dot(cot, w2, 1, 1) * slope).astype(BF)
                    grads[i % 4, k, half, 1] = dot(a, cot, 0, 0).astype(BF)
                    grads[i % 4, k, half, 0] = dot(q, p, 0, 0).astype(BF)
                    part = dot(q, w1, 1, 1)
                    add = part if add is None else add + part
                state[...] += add

        @pl.when(i + 2 < L)
        def _():
            load1(L - 3 - i).start()
            load2(L - 3 - i).start()

        @pl.when(i == L)
        def _():
            low[...] = state[...].astype(BF)

            @pl.loop(0, 3)
            def _(k):
                for half in range(2):
                    cols = pl.ds(pl.multiple_of(k * 768 + half * 384, 384), 384)
                    gin[k, half] = dot(xb[:, cols], low[...], 0, 0).astype(BF)

        end(i)

    last, entry = job(L - 1), job_in()
    entry.follow(5, 7, 6)
    last.follow(7, 8)
    entry.follow(7, 8)
    entry.wait(6)
    last.wait(8)
    entry.wait(8)
    put(L - 1, 0, False)
    put(L - 1, 1, False)
    base = 2 * NC * len(GROUPS)
    leave = []
    for n, ref in enumerate((hin, min_, fin, bin_, far, both)):
        for k in range(NC):
            dst = out[base + n * NC + k]
            leave.append(pltpu.make_async_copy(ref.at[k], dst if n < 4 else dst.at[0], hx.at[n, k]))
    for c in leave:
        c.start()
    for c in leave:
        c.wait()


def first_call(scale, w_in, w_up, w_down, x_rows, y_rows):
    sds = jax.ShapeDtypeStruct
    shapes = [sds((count, 2, 128, D), BF) for _, count in GROUPS for _ in range(2 * NC)]
    shapes += [sds((192, D), BF)] * (4 * NC) + [sds((1, 2, 128, D), BF)] * (2 * NC)
    dma = pltpu.SemaphoreType.DMA
    scratch = [
        pltpu.VMEM((2, D, FF), F32), pltpu.VMEM((2, FF, D), F32),
        pltpu.VMEM((L, ROWS, D), BF),
        pltpu.VMEM((4, NC, 2, 2, 256, D), BF), pltpu.VMEM((NC, 2, 384, D), BF),
        pltpu.VMEM((2, NC, 2, 256, D), BF), pltpu.VMEM((2, NC, 2, 128, D), BF),
        pltpu.VMEM((2, NC, 2, 64, D), BF), pltpu.VMEM((2, NC, 2, 32, D), BF),
        pltpu.VMEM((NC, 384, D), BF), pltpu.VMEM((NC, 192, D), BF),
        pltpu.VMEM((NC, 96, D), BF), pltpu.VMEM((NC, 48, D), BF),
        pltpu.VMEM((4, NC, 2, 128, D), BF), pltpu.VMEM((3, NC, 2, 128, D), BF),
        pltpu.VMEM((NC, 2, 128, D), BF), pltpu.VMEM((NC, 2, 128, D), BF),
        pltpu.VMEM((NC, 192, D), BF), pltpu.VMEM((NC, 192, D), BF),
        pltpu.VMEM((NC, 192, D), BF), pltpu.VMEM((NC, 192, D), BF),
        pltpu.VMEM((ROWS, E), BF), pltpu.VMEM((ROWS, D), BF),
        pltpu.VMEM((ROWS, D), F32), pltpu.VMEM((ROWS, D), BF),
        dma((9, 2, NC)), dma((9, 2, NC)), dma((9, NC)), dma((9, NC)),
        dma((2,)), dma((2,)), dma((2,)), dma((2, 2, NC)), dma((6, NC)),
    ]
    res = pl.pallas_call(
        functools.partial(first_kernel, scale),
        out_shape=shapes,
        in_specs=[ANY] * 5,
        out_specs=[ANY] * len(shapes),
        scratch_shapes=scratch,
        name="train_step",
        cost_estimate=pl.CostEstimate(flops=75 * 10**9, bytes_accessed=200 * 10**6, transcendentals=0),
        compiler_params=pltpu.CompilerParams(collective_id=0, has_side_effects=True, vmem_limit_bytes=67043328),
    )(w_in, w_up, w_down, x_rows, y_rows)
    take3 = lambda n: res[n * NC:(n + 1) * NC]
    n = 2 * len(GROUPS)
    pairs = [(take3(2 * g), take3(2 * g + 1)) for g in range(len(GROUPS))]
    return pairs, [take3(n + r) for r in range(6)]


def layers_kernel(eta, first, count, head, *refs):
    n_parts = 4 * NC * (2 if head else 1)
    parts = refs[:4 * NC]
    w1_hbm, m1_hbm, w2_hbm, m2_hbm, h_hbm = refs[n_parts:n_parts + 5]
    rest = refs[n_parts + 5 + (2 if head else 4):]
    if head:
        parts_in = refs[4 * NC:n_parts]
        w_hbm, m_hbm = refs[n_parts + 5:n_parts + 7]
        new_win, new_min = rest[:2]
        rest = rest[2:]
    new_w1, new_m1, new_w2, new_m2, h_out = rest[:5]
    v1, v2, gv, hv, av, gs, ins, outs, hs = rest[5:14]
    core, _, bits, _ = position()

    def load(n, y):
        s = n % 3
        res = [pltpu.make_async_copy(src.at[first + n], dst.at[s, z], ins.at[s, y, z])
               for yy, (a, b, dst) in enumerate(((w1_hbm, m1_hbm, v1), (w2_hbm, m2_hbm, v2)))
               for z, src in enumerate((a, b)) if yy == y]
        for k in range(NC):
            for r in range(4):
                c = core if r < 2 else 1 - core
                b = bits[k] if r % 2 == 0 else 1 - bits[k]
                at = pl.multiple_of(k * 512 + c * 256 + b * 128, 128)
                res.append(pltpu.make_async_copy(parts[k * 4 + r].at[n, y], gv.at[s, y, pl.ds(at, 128), :],
                                                 gs.at[s, y, k, r]))
        return res

    def store(n, y):
        s = n % 3
        return [pltpu.make_async_copy(src.at[s, z], dst.at[first + n], outs.at[s, y, z])
                for yy, (src, a, b) in enumerate(((v1, new_w1, new_m1), (v2, new_w2, new_m2)))
                for z, dst in enumerate((a, b)) if yy == y]

    load_h = pltpu.make_async_copy(h_hbm, rest[14] if head else hv, hs.at[0])
    if head:
        xv, wv, mv, gi, gsi, insi, outsi = rest[14:]

        def load_in(k):
            rows = pl.ds(k * 768, 768)
            res = [pltpu.make_async_copy(w_hbm.at[rows], wv.at[rows], insi.at[0, k]),
                   pltpu.make_async_copy(m_hbm.at[rows], mv.at[rows], insi.at[1, k])]
            for r in range(4):
                c = core if r < 2 else 1 - core
                b = bits[k] if r % 2 == 0 else 1 - bits[k]
                at = pl.multiple_of(k * 768 + c * 384 + b * 192, 16)
                res.append(pltpu.make_async_copy(parts_in[k * 4 + r], gi.at[pl.ds(at, 192)], gsi.at[k, r]))
            return res

        def store_in(k):
            rows = pl.ds(k * 768, 768)
            return [pltpu.make_async_copy(wv.at[rows], new_win.at[rows], outsi.at[0, k]),
                    pltpu.make_async_copy(mv.at[rows], new_min.at[rows], outsi.at[1, k])]

        for c in load_in(0) + [load_h] + load_in(1) + load_in(2) + load(0, 0) + load(0, 1):
            c.start()
        for k in range(NC):
            for c in load_in(k) + ([load_h] if k == 0 else []):
                c.wait()
            rows = slice(k * 768, k * 768 + 768)
            m = MOMENTUM * mv[rows, :] + gi[rows, :].astype(F32)
            w = wv[rows, :] - eta * m
            mv[rows, :] = m
            wv[rows, :] = w
            for c in store_in(k):
                c.start()
            part = dot(xv[:, rows], w.astype(BF), 1, 0)
            hv[...] = part if k == 0 else hv[...] + part
    else:
        for c in load(0, 0) + [load_h] + load(0, 1):
            c.start()
        load_h.wait()

    @pl.loop(0, count)
    def _(n):
        s = n % 3

        @pl.when(n >= 2)
        def _():
            for c in store(n - 2, 0) + store(n - 2, 1):
                c.wait()

        @pl.when(n + 1 < count)
        def _():
            for c in load(n + 1, 0) + load(n + 1, 1):
                c.start()

        for c in load(n, 0):
            c.wait()
        p = hv[...].astype(BF)

        @pl.loop(0, 3)
        def _(j):
            for half in range(2):
                cols = pl.ds(pl.multiple_of(j * 512 + half * 256, 256), 256)
                m1 = MOMENTUM * v1[s, 1, :, cols] + gv[s, 0, cols, :].astype(F32).T
                w1 = v1[s, 0, :, cols] - eta * m1
                v1[s, 1, :, cols] = m1
                v1[s, 0, :, cols] = w1
                av[:, cols] = gelu_low(dot(p, w1.astype(BF), 1, 0))

        for c in store(n, 0):
            c.start()
        for c in load(n, 1):
            c.wait()

        @pl.loop(0, 3)
        def _(j):
            cols = pl.ds(pl.multiple_of(j * 512, 512), 512)
            m2 = MOMENTUM * v2[s, 1, cols, :] + gv[s, 1, cols, :].astype(F32)
            w2 = v2[s, 0, cols, :] - eta * m2
            v2[s, 1, cols, :] = m2
            v2[s, 0, cols, :] = w2
            hv[...] += dot(av[:, cols], w2.astype(BF), 1, 0)

        for c in store(n, 1):
            c.start()

    give_h = pltpu.make_async_copy(hv, h_out, hs.at[1])
    give_h.start()
    for n in range(max(0, count - 2), count):
        for c in store(n, 0) + store(n, 1):
            c.wait()
    if head:
        for k in range(NC):
            for c in store_in(k):
                c.wait()
    give_h.wait()


def layers_call(eta, first, count, parts, arrays, h, made, head=None):
    sds = jax.ShapeDtypeStruct
    dma = pltpu.SemaphoreType.DMA
    flat = [p for k in range(NC) for p in parts[k]]
    if head:
        flat += [p for k in range(NC) for p in head[0][k]]
    n = len(flat)
    more = list(head[1:]) if head else list(made)
    shapes = [sds((E, D), F32)] * 2 if head else []
    shapes += [sds((L, D, FF), F32), sds((L, D, FF), F32), sds((L, FF, D), F32), sds((L, FF, D), F32),
               sds((ROWS, D), F32)]
    scratch = [pltpu.VMEM((3, 2, D, FF), F32), pltpu.VMEM((3, 2, FF, D), F32),
               pltpu.VMEM((3, 2, FF, D), BF), pltpu.VMEM((ROWS, D), F32), pltpu.VMEM((ROWS, FF), BF),
               dma((3, 2, NC, 4)), dma((3, 2, 2)), dma((3, 2, 2)), dma((2,))]
    if head:
        scratch += [pltpu.VMEM((ROWS, E), BF), pltpu.VMEM((E, D), F32), pltpu.VMEM((E, D), F32),
                    pltpu.VMEM((E, D), BF), dma((NC, 4)), dma((2, NC)), dma((2, NC))]
    return pl.pallas_call(
        functools.partial(layers_kernel, eta, first, count, head is not None),
        out_shape=shapes,
        in_specs=[ANY] * (n + 5 + len(more)),
        out_specs=[ANY] * len(shapes),
        input_output_aliases={} if head else {n + 5 + r: r for r in range(4)},
        scratch_shapes=scratch,
        cost_estimate=pl.CostEstimate(flops=count * 6 * 10**9, bytes_accessed=count * 21 * 10**6, transcendentals=0),
        compiler_params=pltpu.CompilerParams(vmem_limit_bytes=67043328),
    )(*flat, *arrays, h, *more)


def solution(mesh):
    group_size = mesh.shape["data"]

    def swap(v, bit):
        return lax.ppermute(v, "data", [(d, d ^ bit) for d in range(group_size)])

    def far_half(own):
        res = []
        for k in range(NC):
            res.append(swap(own[k], 2 << k))
        return res

    def complete(own, mate, other, after):
        other = lax.optimization_barrier((*other, after))[:NC]
        res = []
        for k in range(NC):
            res.append((own[k], other[k], mate[k], swap(other[k], 1)))
        return res

    def device_steps(w_in, w_up, w_down, mom_in, mom_up, mom_down, x_now, y_now, x_next, y_next):
        eta = 4.0 * D / (FF * (L + 1))
        scale = 1.0 / (ROWS * group_size * D)
        pairs, (own, mate, other, both, other0, both0) = first_call(scale, w_in, w_up, w_down, x_now, y_now)
        parts_in = [(own[k], other[k], mate[k], both[k]) for k in range(NC)]
        parts = [[(pairs[0][0][k], other0[k], pairs[0][1][k], both0[k]) for k in range(NC)]]
        others = [far_half(pair[0]) for pair in pairs[1:]]
        arrays = (w_up, mom_up, w_down, mom_down)
        after = pairs[0][0][0]
        for g, (first, count) in enumerate(GROUPS):
            if g == 0:
                new_w_in, new_mom_in, *made, h = layers_call(eta, first, count, parts[0], arrays, x_next, None,
                                                             (parts_in, w_in, mom_in))
                after = h
                continue
            parts.append(complete(*pairs[g], others[g - 1], h if g == 2 else after))
            after = h
            *made, h = layers_call(eta, first, count, parts[g], arrays, h, made)
        new_w_up, new_mom_up, new_w_down, new_mom_down = made
        loss = jnp.sum(jnp.square(h - y_next.astype(F32)), axis=1) / (2 * D)
        return (new_w_in, new_w_up, new_w_down, new_mom_in, new_mom_up, new_mom_down, loss, h)

    param_spec = P()
    row_spec = P("data", None)
    return jax.shard_map(
        device_steps,
        mesh=mesh,
        in_specs=(param_spec,) * 6 + (row_spec,) * 4,
        out_specs=(param_spec,) * 6 + (P("data"), row_spec),
        check_vma=False,
    )
```

profile of v0, /device:TPU:0, one launch (start us, length us, event | category | flops | bytes accessed | tf_op | source)
XLA Modules:
  0.0 427.7 jit_solution(2083190924611609767)
XLA Ops:
  0.6 248.5 %train_step.1 = (bf16[1,2,128,384]{3,2,1,0:T(8,128)(2,1)}, bf16[1,2,128,384]{3,2,1,0:T(8,128)(2,1)}, bf16[1,2,128,384]{3,2,1,0:T(8,128)(2,1)}, bf16[1,2,128,384]...) custom-call(f32[2304,384]{1,0:T(8,128)} %refs_29_.1, ...), custom_call_target="tpu_custom_call" | custom-call | flops 74999996416 | bytes 200000000 | tf_op jit(solution)/shard_map/train_step/pallas_call | solution.py:354
  249.1 1.3 collective-permute-start.3
  250.4 0.7 collective-permute-start.4
  251.2 1.4 collective-permute-start.5
  252.6 0.6 collective-permute-start.12
  253.2 15.7 %shard_map.161 = (f32[2304,384]{1,0:T(8,128)}, f32[2304,384]{1,0:T(8,128)}, f32[16,384,1536]{2,1,0:T(8,128)}, f32[16,384,1536]{2,1,0:T(8,128)}, f32[16,1536,384]...) custom-call(bf16[1,2,128,384]{3,2,1,0:T(8,128)(2,1)} %get-tuple-element.81.refs_0_, ...), custom_call_target="tpu_custom_call" | custom-call | flops 6000000000 | bytes 21000000 | tf_op jit(solution)/shard_map/pallas_call | solution.py:517
  268.9 0.0 collective-permute-done.4.refs_5_
  268.9 0.0 collective-permute-done.5.refs_9_
  268.9 0.0 collective-permute-start.6
  269.0 0.5 collective-permute-start.7
  269.5 0.1 collective-permute-start.8
  269.5 1.3 collective-permute-start.13
  270.8 15.3 %collective-permute-done.12.refs_1_ = bf16[5,2,128,384]{3,2,1,0:T(8,128)(2,1)} collective-permute-done((bf16[5,2,128,384]{3,2,1,0:T(8,128)(2,1)}, bf16[5,2,128,384]{3,2,1,0:T(8,128)(2,1)}, u32[]{:S(2)}, u32[]{:S(2)}) %collective-permute-start.12) | collective-permute-done | bytes 983072 | tf_op jit(solution)/shard_map/ppermute | solution.py:533
  286.1 1.3 collective-permute-start.14
  287.5 0.0 collective-permute-done.6.refs_3_
  287.5 0.7 collective-permute-start
  288.2 1.4 collective-permute-start.1
  289.6 0.6 collective-permute-start.2
  290.2 23.5 %shard_map.162 = (f32[16,384,1536]{2,1,0:T(8,128)}, f32[16,384,1536]{2,1,0:T(8,128)}, f32[16,1536,384]{2,1,0:T(8,128)}, f32[16,1536,384]{2,1,0:T(8,128)}, f32[512,384]{1,0:T(8,128)}) custom-call(bf16[3,2,128,384]{3,2,1,0:T(8,128)(2,1)} %get-tuple-element.109.refs_0_, ...), custom_call_target="tpu_custom_call", output_to_operand_aliasing={{0}: (17, {}), {1}: (18, {}), {2}: (19, {}), {3}: (20, {})} | custom-call | flops 17999998976 | bytes 63000000 | tf_op jit(solution)/shard_map/pallas_call | solution.py:517
  313.7 0.0 collective-permute-done.13.refs_5_
  313.7 0.0 collective-permute-start.15
  313.8 0.5 collective-permute-start.16
  314.3 4.8 %collective-permute-done.refs_1_ = bf16[7,2,128,384]{3,2,1,0:T(8,128)(2,1)} collective-permute-done((bf16[7,2,128,384]{3,2,1,0:T(8,128)(2,1)}, bf16[7,2,128,384]{3,2,1,0:T(8,128)(2,1)}, u32[]{:S(2)}, u32[]{:S(2)}) %collective-permute-start) | collective-permute-done | bytes 1376288 | tf_op jit(solution)/shard_map/ppermute | solution.py:533
  319.1 4.3 %collective-permute-done.1.refs_5_ = bf16[7,2,128,384]{3,2,1,0:T(8,128)(2,1)} collective-permute-done((bf16[7,2,128,384]{3,2,1,0:T(8,128)(2,1)}, bf16[7,2,128,384]{3,2,1,0:T(8,128)(2,1)}, u32[]{:S(2)}, u32[]{:S(2)}) %collective-permute-start.1) | collective-permute-done | bytes 1376288 | tf_op jit(solution)/shard_map/ppermute | solution.py:533
  323.4 15.7 %collective-permute-done.2.refs_9_ = bf16[7,2,128,384]{3,2,1,0:T(8,128)(2,1)} collective-permute-done((bf16[7,2,128,384]{3,2,1,0:T(8,128)(2,1)}, bf16[7,2,128,384]{3,2,1,0:T(8,128)(2,1)}, u32[]{:S(2)}, u32[]{:S(2)}) %collective-permute-start.2) | collective-permute-done | bytes 1376288 | tf_op jit(solution)/shard_map/ppermute | solution.py:533
  339.1 0.0 collective-permute-start.10
  339.1 0.5 collective-permute-start.11
  339.6 0.0 collective-permute-start.9
  339.7 36.1 %shard_map.163 = (f32[16,384,1536]{2,1,0:T(8,128)}, f32[16,384,1536]{2,1,0:T(8,128)}, f32[16,1536,384]{2,1,0:T(8,128)}, f32[16,1536,384]{2,1,0:T(8,128)}, f32[512,384]{1,0:T(8,128)}) custom-call(bf16[5,2,128,384]{3,2,1,0:T(8,128)(2,1)} %get-tuple-element.130.refs_0_, ...), custom_call_target="tpu_custom_call", output_to_operand_aliasing={{0}: (17, {}), {1}: (18, {}), {2}: (19, {}), {3}: (20, {})} | custom-call | flops 30000001024 | bytes 105000000 | tf_op jit(solution)/shard_map/pallas_call | solution.py:517
  375.8 49.9 %shard_map.164 = (f32[16,384,1536]{2,1,0:T(8,128)}, f32[16,384,1536]{2,1,0:T(8,128)}, f32[16,1536,384]{2,1,0:T(8,128)}, f32[16,1536,384]{2,1,0:T(8,128)}, f32[512,384]{1,0:T(8,128)}) custom-call(bf16[7,2,128,384]{3,2,1,0:T(8,128)(2,1)} %get-tuple-element.106.refs_0_, ...), custom_call_target="tpu_custom_call", output_to_operand_aliasing={{0}: (17, {}), {1}: (18, {}), {2}: (19, {}), {3}: (20, {})} | custom-call | flops 41999998976 | bytes 147000000 | tf_op jit(solution)/shard_map/pallas_call | solution.py:517
  425.7 1.4 multiply_reduce_fusion
  427.1 0.6 broadcast_multiply_fusion
  (11 shorter events, 0.0 us)
Async XLA Ops:
  249.1 19.8 %collective-permute-start.3 = (bf16[3,2,128,384]{3,2,1,0:T(8,128)(2,1)}, bf16[3,2,128,384]{3,2,1,0:T(8,128)(2,1)}, u32[]{:S(2)}, u32[]{:S(2)}) collective-permute-start(bf16[3,2,128,384]{3,2,1,0:T(8,128)(2,1)} %get-tuple-element.109.refs_0_), channel_id=1, source_target_pairs={{0,2},{1,3},{2,0},{3,1},{4,6},{5,7},{6,4},{7,5},{8,10},{9,11},{10,... | collective-permute-start | bytes 1769480 | tf_op jit(solution)/shard_map/ppermute | solution.py:533
  250.4 18.5 %collective-permute-start.4 = (bf16[3,2,128,384]{3,2,1,0:T(8,128)(2,1)}, bf16[3,2,128,384]{3,2,1,0:T(8,128)(2,1)}, u32[]{:S(2)}, u32[]{:S(2)}) collective-permute-start(bf16[3,2,128,384]{3,2,1,0:T(8,128)(2,1)} %get-tuple-element.110.refs_4_), channel_id=1, source_target_pairs={{0,4},{1,5},{2,6},{3,7},{4,0},{5,1},{6,2},{7,3},{8,12},{9,13},{10,... | collective-permute-start | bytes 1769480 | tf_op jit(solution)/shard_map/ppermute | solution.py:533
  251.2 17.7 %collective-permute-start.5 = (bf16[3,2,128,384]{3,2,1,0:T(8,128)(2,1)}, bf16[3,2,128,384]{3,2,1,0:T(8,128)(2,1)}, u32[]{:S(2)}, u32[]{:S(2)}) collective-permute-start(bf16[3,2,128,384]{3,2,1,0:T(8,128)(2,1)} %get-tuple-element.111.refs_8_), channel_id=1, source_target_pairs={{0,8},{1,9},{2,10},{3,11},{4,12},{5,13},{6,14},{7,15},{8,0},{9,1},... | collective-permute-start | bytes 1769480 | tf_op jit(solution)/shard_map/ppermute | solution.py:533
  252.6 33.6 %collective-permute-start.12 = (bf16[5,2,128,384]{3,2,1,0:T(8,128)(2,1)}, bf16[5,2,128,384]{3,2,1,0:T(8,128)(2,1)}, u32[]{:S(2)}, u32[]{:S(2)}) collective-permute-start(bf16[5,2,128,384]{3,2,1,0:T(8,128)(2,1)} %get-tuple-element.130.refs_0_), channel_id=1, source_target_pairs={{0,2},{1,3},{2,0},{3,1},{4,6},{5,7},{6,4},{7,5},{8,10},{9,11},{10,... | collective-permute-start | bytes 2949128 | tf_op jit(solution)/shard_map/ppermute | solution.py:533
  268.9 18.5 %collective-permute-start.6 = (bf16[3,2,128,384]{3,2,1,0:T(8,128)(2,1)}, bf16[3,2,128,384]{3,2,1,0:T(8,128)(2,1)}, u32[]{:S(2)}, u32[]{:S(2)}) collective-permute-start(bf16[3,2,128,384]{3,2,1,0:T(8,128)(2,1)} %collective-permute-done.3.refs_1_), channel_id=1, source_target_pairs={{0,1},{1,0},{2,3},{3,2},{4,5},{5,4},{6,7},{7,6},{8,9},{9,8},{10,11... | collective-permute-start | bytes 1769480 | tf_op jit(solution)/shard_map/ppermute | solution.py:533
  269.0 19.2 %collective-permute-start.7 = (bf16[3,2,128,384]{3,2,1,0:T(8,128)(2,1)}, bf16[3,2,128,384]{3,2,1,0:T(8,128)(2,1)}, u32[]{:S(2)}, u32[]{:S(2)}) collective-permute-start(bf16[3,2,128,384]{3,2,1,0:T(8,128)(2,1)} %collective-permute-done.4.refs_5_), channel_id=1, source_target_pairs={{0,1},{1,0},{2,3},{3,2},{4,5},{5,4},{6,7},{7,6},{8,9},{9,8},{10,11... | collective-permute-start | bytes 1769480 | tf_op jit(solution)/shard_map/ppermute | solution.py:533
  269.5 20.1 %collective-permute-start.8 = (bf16[3,2,128,384]{3,2,1,0:T(8,128)(2,1)}, bf16[3,2,128,384]{3,2,1,0:T(8,128)(2,1)}, u32[]{:S(2)}, u32[]{:S(2)}) collective-permute-start(bf16[3,2,128,384]{3,2,1,0:T(8,128)(2,1)} %collective-permute-done.5.refs_9_), channel_id=1, source_target_pairs={{0,1},{1,0},{2,3},{3,2},{4,5},{5,4},{6,7},{7,6},{8,9},{9,8},{10,11... | collective-permute-start | bytes 1769480 | tf_op jit(solution)/shard_map/ppermute | solution.py:533
  269.5 44.2 %collective-permute-start.13 = (bf16[5,2,128,384]{3,2,1,0:T(8,128)(2,1)}, bf16[5,2,128,384]{3,2,1,0:T(8,128)(2,1)}, u32[]{:S(2)}, u32[]{:S(2)}) collective-permute-start(bf16[5,2,128,384]{3,2,1,0:T(8,128)(2,1)} %get-tuple-element.131.refs_4_), channel_id=1, source_target_pairs={{0,4},{1,5},{2,6},{3,7},{4,0},{5,1},{6,2},{7,3},{8,12},{9,13},{10,... | collective-permute-start | bytes 2949128 | tf_op jit(solution)/shard_map/ppermute | solution.py:533
  286.1 27.6 %collective-permute-start.14 = (bf16[5,2,128,384]{3,2,1,0:T(8,128)(2,1)}, bf16[5,2,128,384]{3,2,1,0:T(8,128)(2,1)}, u32[]{:S(2)}, u32[]{:S(2)}) collective-permute-start(bf16[5,2,128,384]{3,2,1,0:T(8,128)(2,1)} %get-tuple-element.132.refs_8_), channel_id=1, source_target_pairs={{0,8},{1,9},{2,10},{3,11},{4,12},{5,13},{6,14},{7,15},{8,0},{9,1},... | collective-permute-start | bytes 2949128 | tf_op jit(solution)/shard_map/ppermute | solution.py:533
  287.5 31.6 %collective-permute-start = (bf16[7,2,128,384]{3,2,1,0:T(8,128)(2,1)}, bf16[7,2,128,384]{3,2,1,0:T(8,128)(2,1)}, u32[]{:S(2)}, u32[]{:S(2)}) collective-permute-start(bf16[7,2,128,384]{3,2,1,0:T(8,128)(2,1)} %get-tuple-element.106.refs_0_), channel_id=1, source_target_pairs={{0,2},{1,3},{2,0},{3,1},{4,6},{5,7},{6,4},{7,5},{8,10},{9,11},{10,... | collective-permute-start | bytes 4128776 | tf_op jit(solution)/shard_map/ppermute | solution.py:533
  288.2 35.2 %collective-permute-start.1 = (bf16[7,2,128,384]{3,2,1,0:T(8,128)(2,1)}, bf16[7,2,128,384]{3,2,1,0:T(8,128)(2,1)}, u32[]{:S(2)}, u32[]{:S(2)}) collective-permute-start(bf16[7,2,128,384]{3,2,1,0:T(8,128)(2,1)} %get-tuple-element.107.refs_4_), channel_id=1, source_target_pairs={{0,4},{1,5},{2,6},{3,7},{4,0},{5,1},{6,2},{7,3},{8,12},{9,13},{10,... | collective-permute-start | bytes 4128776 | tf_op jit(solution)/shard_map/ppermute | solution.py:533
  289.6 49.6 %collective-permute-start.2 = (bf16[7,2,128,384]{3,2,1,0:T(8,128)(2,1)}, bf16[7,2,128,384]{3,2,1,0:T(8,128)(2,1)}, u32[]{:S(2)}, u32[]{:S(2)}) collective-permute-start(bf16[7,2,128,384]{3,2,1,0:T(8,128)(2,1)} %get-tuple-element.108.refs_8_), channel_id=1, source_target_pairs={{0,8},{1,9},{2,10},{3,11},{4,12},{5,13},{6,14},{7,15},{8,0},{9,1},... | collective-permute-start | bytes 4128776 | tf_op jit(solution)/shard_map/ppermute | solution.py:533
  313.7 25.9 %collective-permute-start.15 = (bf16[5,2,128,384]{3,2,1,0:T(8,128)(2,1)}, bf16[5,2,128,384]{3,2,1,0:T(8,128)(2,1)}, u32[]{:S(2)}, u32[]{:S(2)}) collective-permute-start(bf16[5,2,128,384]{3,2,1,0:T(8,128)(2,1)} %collective-permute-done.12.refs_1_), channel_id=1, source_target_pairs={{0,1},{1,0},{2,3},{3,2},{4,5},{5,4},{6,7},{7,6},{8,9},{9,8},{10,11... | collective-permute-start | bytes 2949128 | tf_op jit(solution)/shard_map/ppermute | solution.py:533
  313.8 25.9 %collective-permute-start.16 = (bf16[5,2,128,384]{3,2,1,0:T(8,128)(2,1)}, bf16[5,2,128,384]{3,2,1,0:T(8,128)(2,1)}, u32[]{:S(2)}, u32[]{:S(2)}) collective-permute-start(bf16[5,2,128,384]{3,2,1,0:T(8,128)(2,1)} %collective-permute-done.13.refs_5_), channel_id=1, source_target_pairs={{0,1},{1,0},{2,3},{3,2},{4,5},{5,4},{6,7},{7,6},{8,9},{9,8},{10,11... | collective-permute-start | bytes 2949128 | tf_op jit(solution)/shard_map/ppermute | solution.py:533
  319.1 20.6 %collective-permute-start.17 = (bf16[5,2,128,384]{3,2,1,0:T(8,128)(2,1)}, bf16[5,2,128,384]{3,2,1,0:T(8,128)(2,1)}, u32[]{:S(2)}, u32[]{:S(2)}) collective-permute-start(bf16[5,2,128,384]{3,2,1,0:T(8,128)(2,1)} %collective-permute-done.14.refs_9_), channel_id=1, source_target_pairs={{0,1},{1,0},{2,3},{3,2},{4,5},{5,4},{6,7},{7,6},{8,9},{9,8},{10,11... | collective-permute-start | bytes 2949128 | tf_op jit(solution)/shard_map/ppermute | solution.py:533
  339.1 36.6 %collective-permute-start.10 = (bf16[7,2,128,384]{3,2,1,0:T(8,128)(2,1)}, bf16[7,2,128,384]{3,2,1,0:T(8,128)(2,1)}, u32[]{:S(2)}, u32[]{:S(2)}) collective-permute-start(bf16[7,2,128,384]{3,2,1,0:T(8,128)(2,1)} %collective-permute-done.1.refs_5_), channel_id=1, source_target_pairs={{0,1},{1,0},{2,3},{3,2},{4,5},{5,4},{6,7},{7,6},{8,9},{9,8},{10,11... | collective-permute-start | bytes 4128776 | tf_op jit(solution)/shard_map/ppermute | solution.py:533
  339.1 36.6 %collective-permute-start.11 = (bf16[7,2,128,384]{3,2,1,0:T(8,128)(2,1)}, bf16[7,2,128,384]{3,2,1,0:T(8,128)(2,1)}, u32[]{:S(2)}, u32[]{:S(2)}) collective-permute-start(bf16[7,2,128,384]{3,2,1,0:T(8,128)(2,1)} %collective-permute-done.2.refs_9_), channel_id=1, source_target_pairs={{0,1},{1,0},{2,3},{3,2},{4,5},{5,4},{6,7},{7,6},{8,9},{9,8},{10,11... | collective-permute-start | bytes 4128776 | tf_op jit(solution)/shard_map/ppermute | solution.py:533
  339.6 36.1 %collective-permute-start.9 = (bf16[7,2,128,384]{3,2,1,0:T(8,128)(2,1)}, bf16[7,2,128,384]{3,2,1,0:T(8,128)(2,1)}, u32[]{:S(2)}, u32[]{:S(2)}) collective-permute-start(bf16[7,2,128,384]{3,2,1,0:T(8,128)(2,1)} %collective-permute-done.refs_1_), channel_id=1, source_target_pairs={{0,1},{1,0},{2,3},{3,2},{4,5},{5,4},{6,7},{7,6},{8,9},{9,8},{10,11... | collective-permute-start | bytes 4128776 | tf_op jit(solution)/shard_map/ppermute | solution.py:533
where the time goes:
time: 428 us
  Pallas kernels  374 us (87%)
  waiting for transfers between devices  40.2 us (9%)
  starting transfers between devices  11.1 us (3%)
    pallas_call x1, Pallas kernels, first_call(): pl.pallas_call(functools.partial(first_kernel, scale), out_shape=shapes,...  248 us
    pallas_call x4, Pallas kernels, layers_call(): pl.pallas_call(functools.partial(layers_kernel, eta, first, count, head i...  125 us
    ppermute x18, waiting for transfers between devices, swap(): return lax.ppermute(v, 'data', [(d, d ^ bit) for d in range(group_size)])  40.2 us
    ppermute x18, starting transfers between devices, swap(): return lax.ppermute(v, 'data', [(d, d ^ bit) for d in range(group_size)])  11.1 us
  transfers between devices with their start and end apart: 18, of which 4 were waited for; matrix products, arithmetic and copies ran while one was open for 0% of the time, Pallas kernels for 18%

commit v1 on v0

--- a/solution.py
+++ b/solution.py
@@ -16,7 +16,7 @@
 VM = pl.BlockSpec(memory_space=pltpu.VMEM)
 L, D, FF, E, ROWS = 16, 384, 1536, 2304, 512
 NC = 3
-GROUPS = ((0, 1), (1, 3), (4, 5), (9, 7))
+GROUPS = ((0, 1), (1, 2), (3, 4), (7, 9))
 N_OUT = NC * (2 * len(GROUPS) + 6)
 KAPPA = 0.7978845608028654
 
@@ -134,7 +134,6 @@
     barrier = pltpu.get_barrier_semaphore()
     for dev in [pos[1]] + pos[3]:
         pl.semaphore_signal(barrier, inc=1, device_id=(dev,), device_id_type=MESH)
-    pl.semaphore_wait(barrier, 4)
 
     def load1(l):
         return pltpu.make_async_copy(w_up.at[l], st1.at[l % 2], ld1.at[l % 2])
@@ -168,7 +167,7 @@
         load1(l).wait()
         load2(l).wait()
 
-        for j in range(3):
+        for j in range(NC):
             cols = slice(j * 512, j * 512 + 512)
             a = gelu_low(dot(p, st1[slot, :, cols].astype(BF), 1, 0))
             state[...] += dot(a, st2[slot, cols, :].astype(BF), 1, 0)
@@ -178,6 +177,7 @@
             load1(l + 2).start()
             load2(l + 2).start()
 
+    pl.semaphore_wait(barrier, 4)
     load_y.wait()
     state[...] = (state[...] - yb[...].astype(F32)) * scale
 
@@ -252,8 +252,6 @@
             job(i - 5).wait(6)
             put(i - 5, 1, True)
 
-        during(i, 0, lambda: job(i).start(0))
-        pl.when(i == L)(lambda: job_in().start(0))
 
     @pl.loop(0, L + 5)
     def _(i):
@@ -266,11 +264,10 @@
 
             low[...] = state[...].astype(BF)
 
-        @pl.loop(0, 3)
+        @pl.loop(0, NC)
         def _(k):
-            @pl.when(k == 1)
-            def _():
-                middle(i)
+            pl.when(k == 0)(lambda: middle(i))
+            pl.when(k == 2)(lambda: end(i))
 
             @pl.when(i < L)
             def _():
@@ -290,6 +287,7 @@
                     part = dot(q, w1, 1, 1)
                     add = part if add is None else add + part
                 state[...] += add
+                job(i).halving(k, 0).start()
 
         @pl.when(i + 2 < L)
         def _():
@@ -300,13 +298,12 @@
         def _():
             low[...] = state[...].astype(BF)
 
-            @pl.loop(0, 3)
+            @pl.loop(0, NC)
             def _(k):
                 for half in range(2):
                     cols = pl.ds(pl.multiple_of(k * 768 + half * 384, 384), 384)
                     gin[k, half] = dot(xb[:, cols], low[...], 0, 0).astype(BF)
-
-        end(i)
+                job_in().halving(k, 0).start()
 
     last, entry = job(L - 1), job_in()
     entry.follow(5, 7, 6)
@@ -343,13 +340,10 @@
         pltpu.VMEM((NC, 384, D), BF), pltpu.VMEM((NC, 192, D), BF),
         pltpu.VMEM((NC, 96, D), BF), pltpu.VMEM((NC, 48, D), BF),
         pltpu.VMEM((4, NC, 2, 128, D), BF), pltpu.VMEM((3, NC, 2, 128, D), BF),
-        pltpu.VMEM((NC, 2, 128, D), BF), pltpu.VMEM((NC, 2, 128, D), BF),
-        pltpu.VMEM((NC, 192, D), BF), pltpu.VMEM((NC, 192, D), BF),
-        pltpu.VMEM((NC, 192, D), BF), pltpu.VMEM((NC, 192, D), BF),
+        *[pltpu.VMEM((NC, 2, 128, D), BF)] * 2, *[pltpu.VMEM((NC, 192, D), BF)] * 4,
         pltpu.VMEM((ROWS, E), BF), pltpu.VMEM((ROWS, D), BF),
         pltpu.VMEM((ROWS, D), F32), pltpu.VMEM((ROWS, D), BF),
-        dma((9, 2, NC)), dma((9, 2, NC)), dma((9, NC)), dma((9, NC)),
-        dma((2,)), dma((2,)), dma((2,)), dma((2, 2, NC)), dma((6, NC)),
+        *[dma((9, 2, NC))] * 2, *[dma((9, NC))] * 2, *[dma((2,))] * 3, dma((2, 2, NC)), dma((6, NC)),
     ]
     res = pl.pallas_call(
         functools.partial(first_kernel, scale),
@@ -367,6 +361,12 @@
     return pairs, [take3(n + r) for r in range(6)]
 
 
+def place(core, bits, k, r, size):
+    c = core if r < 2 else 1 - core
+    b = bits[k] if r % 2 == 0 else 1 - bits[k]
+    return pl.ds(pl.multiple_of((k * 4 + c * 2 + b) * size, 16), size)
+
+
 def layers_kernel(eta, first, count, head, *refs):
     n_parts = 4 * NC * (2 if head else 1)
     parts = refs[:4 * NC]
@@ -388,11 +388,8 @@
                for z, src in enumerate((a, b)) if yy == y]
         for k in range(NC):
             for r in range(4):
-                c = core if r < 2 else 1 - core
-                b = bits[k] if r % 2 == 0 else 1 - bits[k]
-                at = pl.multiple_of(k * 512 + c * 256 + b * 128, 128)
-                res.append(pltpu.make_async_copy(parts[k * 4 + r].at[n, y], gv.at[s, y, pl.ds(at, 128), :],
-                                                 gs.at[s, y, k, r]))
+                rows = place(core, bits, k, r, 128)
+                res.append(pltpu.make_async_copy(parts[k * 4 + r].at[n, y], gv.at[s, y, rows, :], gs.at[s, y, k, r]))
         return res
 
     def store(n, y):
@@ -410,10 +407,8 @@
             res = [pltpu.make_async_copy(w_hbm.at[rows], wv.at[rows], insi.at[0, k]),
                    pltpu.make_async_copy(m_hbm.at[rows], mv.at[rows], insi.at[1, k])]
             for r in range(4):
-                c = core if r < 2 else 1 - core
-                b = bits[k] if r % 2 == 0 else 1 - bits[k]
-                at = pl.multiple_of(k * 768 + c * 384 + b * 192, 16)
-                res.append(pltpu.make_async_copy(parts_in[k * 4 + r], gi.at[pl.ds(at, 192)], gsi.at[k, r]))
+                rows = place(core, bits, k, r, 192)
+                res.append(pltpu.make_async_copy(parts_in[k * 4 + r], gi.at[rows], gsi.at[k, r]))
             return res
 
         def store_in(k):
@@ -458,7 +453,7 @@
             c.wait()
         p = hv[...].astype(BF)
 
-        @pl.loop(0, 3)
+        @pl.loop(0, NC)
         def _(j):
             for half in range(2):
                 cols = pl.ds(pl.multiple_of(j * 512 + half * 256, 256), 256)
@@ -473,7 +468,7 @@
         for c in load(n, 1):
             c.wait()
 
-        @pl.loop(0, 3)
+        @pl.loop(0, NC)
         def _(j):
             cols = pl.ds(pl.multiple_of(j * 512, 512), 512)
             m2 = MOMENTUM * v2[s, 1, cols, :] + gv[s, 1, cols, :].astype(F32)
@@ -506,8 +501,8 @@
     n = len(flat)
     more = list(head[1:]) if head else list(made)
     shapes = [sds((E, D), F32)] * 2 if head else []
-    shapes += [sds((L, D, FF), F32), sds((L, D, FF), F32), sds((L, FF, D), F32), sds((L, FF, D), F32),
-               sds((ROWS, D), F32)]
+    up, down = sds((L, D, FF), F32), sds((L, FF, D), F32)
+    shapes += [up, up, down, down, sds((ROWS, D), F32)]
     scratch = [pltpu.VMEM((3, 2, D, FF), F32), pltpu.VMEM((3, 2, FF, D), F32),
                pltpu.VMEM((3, 2, FF, D), BF), pltpu.VMEM((ROWS, D), F32), pltpu.VMEM((ROWS, FF), BF),
                dma((3, 2, NC, 4)), dma((3, 2, 2)), dma((3, 2, 2)), dma((2,))]
@@ -553,16 +548,15 @@
         parts = [[(pairs[0][0][k], other0[k], pairs[0][1][k], both0[k]) for k in range(NC)]]
         others = [far_half(pair[0]) for pair in pairs[1:]]
         arrays = (w_up, mom_up, w_down, mom_down)
-        after = pairs[0][0][0]
+        parts.append(complete(*pairs[1], others[0], pairs[0][0][0]))
         for g, (first, count) in enumerate(GROUPS):
+            if g in (1, 3):
+                parts.append(complete(*pairs[len(parts)], others[len(parts) - 1], h))
             if g == 0:
                 new_w_in, new_mom_in, *made, h = layers_call(eta, first, count, parts[0], arrays, x_next, None,
                                                              (parts_in, w_in, mom_in))
-                after = h
-                continue
-            parts.append(complete(*pairs[g], others[g - 1], h if g == 2 else after))
-            after = h
-            *made, h = layers_call(eta, first, count, parts[g], arrays, h, made)
+            else:
+                *made, h = layers_call(eta, first, count, parts[g], arrays, h, made)
         new_w_up, new_mom_up, new_w_down, new_mom_down = made
         loss = jnp.sum(jnp.square(h - y_next.astype(F32)), axis=1) / (2 * D)
         return (new_w_in, new_w_up, new_w_down, new_mom_in, new_mom_up, new_mom_down, loss, h)

time: 428 us -> 426 us (level)
  transfers between devices with their start and end apart: 18 -> 18, of which waited for: 4 -> 6; matrix products, arithmetic and copies ran while one was open for 0% -> 0% of each run, Pallas kernels for 18% -> 15%
where the time goes in v1:
time: 426 us
  Pallas kernels  372 us (87%)
  waiting for transfers between devices  40.9 us (10%)
  starting transfers between devices  10.6 us (2%)
    pallas_call x1, Pallas kernels, first_call(): pl.pallas_call(functools.partial(first_kernel, scale), out_shape=shapes,...  246 us
    pallas_call x4, Pallas kernels, layers_call(): pl.pallas_call(functools.partial(layers_kernel, eta, first, count, head i...  126 us
    ppermute x18, waiting for transfers between devices, swap(): return lax.ppermute(v, 'data', [(d, d ^ bit) for d in range(group_size)])  40.9 us
    ppermute x18, starting transfers between devices, swap(): return lax.ppermute(v, 'data', [(d, d ^ bit) for d in range(group_size)])  10.6 us
  transfers between devices with their start and end apart: 18, of which 6 were waited for; matrix products, arithmetic and copies ran while one was open for 0% of the time, Pallas kernels for 15%

profile of v1, /device:TPU:0, one launch (start us, length us, event | category | flops | bytes accessed | tf_op | source)
XLA Modules:
  0.0 426.1 jit_solution(14750474557165213263)
XLA Ops:
  0.6 246.2 %train_step.1 = (bf16[1,2,128,384]{3,2,1,0:T(8,128)(2,1)}, bf16[1,2,128,384]{3,2,1,0:T(8,128)(2,1)}, bf16[1,2,128,384]{3,2,1,0:T(8,128)(2,1)}, bf16[1,2,128,384]...) custom-call(f32[2304,384]{1,0:T(8,128)} %refs_29_.1, ...), custom_call_target="tpu_custom_call" | custom-call | flops 74999996416 | bytes 200000000 | tf_op jit(solution)/shard_map/train_step/pallas_call | solution.py:348
  246.9 0.8 collective-permute-start.3
  247.7 1.4 collective-permute-start.10
  249.0 0.8 collective-permute-start.11
  249.8 1.2 collective-permute-start.9
  251.0 0.7 collective-permute-start.4
  251.7 8.2 %collective-permute-done.10.refs_5_ = bf16[2,2,128,384]{3,2,1,0:T(8,128)(2,1)} collective-permute-done((bf16[2,2,128,384]{3,2,1,0:T(8,128)(2,1)}, bf16[2,2,128,384]{3,2,1,0:T(8,128)(2,1)}, u32[]{:S(2)}, u32[]{:S(2)}) %collective-permute-start.10) | collective-permute-done | bytes 393248 | tf_op jit(solution)/shard_map/ppermute | solution.py:528
  260.0 1.3 collective-permute-start.5
  261.2 0.0 collective-permute-done.11.refs_9_
  261.2 14.2 %collective-permute-done.9.refs_1_ = bf16[2,2,128,384]{3,2,1,0:T(8,128)(2,1)} collective-permute-done((bf16[2,2,128,384]{3,2,1,0:T(8,128)(2,1)}, bf16[2,2,128,384]{3,2,1,0:T(8,128)(2,1)}, u32[]{:S(2)}, u32[]{:S(2)}) %collective-permute-start.9) | collective-permute-done | bytes 393248 | tf_op jit(solution)/shard_map/ppermute | solution.py:528
  275.5 0.5 collective-permute-start.13
  276.0 0.0 collective-permute-done.3.refs_1_
  276.0 0.0 collective-permute-start.14
  276.0 15.7 %shard_map.161 = (f32[2304,384]{1,0:T(8,128)}, f32[2304,384]{1,0:T(8,128)}, f32[16,384,1536]{2,1,0:T(8,128)}, f32[16,384,1536]{2,1,0:T(8,128)}, f32[16,1536,384]...) custom-call(bf16[1,2,128,384]{3,2,1,0:T(8,128)(2,1)} %get-tuple-element.81.refs_0_, ...), custom_call_target="tpu_custom_call" | custom-call | flops 6000000000 | bytes 21000000 | tf_op jit(solution)/shard_map/pallas_call | solution.py:512
  291.7 0.0 collective-permute-done.4.refs_5_
  291.7 0.8 collective-permute-start
  292.5 0.0 collective-permute-done.5.refs_9_
  292.5 1.4 collective-permute-start.1
  293.9 0.5 collective-permute-start.7
  294.4 0.0 collective-permute-start.8
  294.4 16.6 %shard_map.162 = (f32[16,384,1536]{2,1,0:T(8,128)}, f32[16,384,1536]{2,1,0:T(8,128)}, f32[16,1536,384]{2,1,0:T(8,128)}, f32[16,1536,384]{2,1,0:T(8,128)}, f32[512,384]{1,0:T(8,128)}) custom-call(bf16[2,2,128,384]{3,2,1,0:T(8,128)(2,1)} %get-tuple-element.119.refs_0_, ...), custom_call_target="tpu_custom_call", output_to_operand_aliasing={{0}: (17, {}), {1}: (18, {}), {2}: (19, {}), {3}: (20, {})} | custom-call | flops 12000000000 | bytes 42000000 | tf_op jit(solution)/shard_map/pallas_call | solution.py:512
  311.1 0.8 collective-permute-start.2
  311.9 30.7 %shard_map.163 = (f32[16,384,1536]{2,1,0:T(8,128)}, f32[16,384,1536]{2,1,0:T(8,128)}, f32[16,1536,384]{2,1,0:T(8,128)}, f32[16,1536,384]{2,1,0:T(8,128)}, f32[512,384]{1,0:T(8,128)}) custom-call(bf16[4,2,128,384]{3,2,1,0:T(8,128)(2,1)} %get-tuple-element.109.refs_0_, ...), custom_call_target="tpu_custom_call", output_to_operand_aliasing={{0}: (17, {}), {1}: (18, {}), {2}: (19, {}), {3}: (20, {})} | custom-call | flops 24000000000 | bytes 84000000 | tf_op jit(solution)/shard_map/pallas_call | solution.py:512
  342.6 9.8 %collective-permute-done.2.refs_9_ = bf16[9,2,128,384]{3,2,1,0:T(8,128)(2,1)} collective-permute-done((bf16[9,2,128,384]{3,2,1,0:T(8,128)(2,1)}, bf16[9,2,128,384]{3,2,1,0:T(8,128)(2,1)}, u32[]{:S(2)}, u32[]{:S(2)}) %collective-permute-start.2) | collective-permute-done | bytes 1769504 | tf_op jit(solution)/shard_map/ppermute | solution.py:528
  352.4 0.5 collective-permute-start.16
  352.9 0.0 collective-permute-start.17
  352.9 3.5 collective-permute-done.15.refs_3_
  356.4 2.5 collective-permute-done.16.refs_7_
  359.0 2.5 collective-permute-done.17.refs_11_
  361.5 62.6 %shard_map.164 = (f32[16,384,1536]{2,1,0:T(8,128)}, f32[16,384,1536]{2,1,0:T(8,128)}, f32[16,1536,384]{2,1,0:T(8,128)}, f32[16,1536,384]{2,1,0:T(8,128)}, f32[512,384]{1,0:T(8,128)}) custom-call(bf16[9,2,128,384]{3,2,1,0:T(8,128)(2,1)} %get-tuple-element.106.refs_0_, ...), custom_call_target="tpu_custom_call", output_to_operand_aliasing={{0}: (17, {}), {1}: (18, {}), {2}: (19, {}), {3}: (20, {})} | custom-call | flops 54000001024 | bytes 189000000 | tf_op jit(solution)/shard_map/pallas_call | solution.py:512
  424.1 1.4 multiply_reduce_fusion
  425.6 0.6 broadcast_multiply_fusion
  (11 shorter events, 0.0 us)
Async XLA Ops:
  246.9 29.1 %collective-permute-start.3 = (bf16[4,2,128,384]{3,2,1,0:T(8,128)(2,1)}, bf16[4,2,128,384]{3,2,1,0:T(8,128)(2,1)}, u32[]{:S(2)}, u32[]{:S(2)}) collective-permute-start(bf16[4,2,128,384]{3,2,1,0:T(8,128)(2,1)} %get-tuple-element.109.refs_0_), channel_id=1, source_target_pairs={{0,2},{1,3},{2,0},{3,1},{4,6},{5,7},{6,4},{7,5},{8,10},{9,11},{10,... | collective-permute-start | bytes 2359304 | tf_op jit(solution)/shard_map/ppermute | solution.py:528
  247.7 12.3 %collective-permute-start.10 = (bf16[2,2,128,384]{3,2,1,0:T(8,128)(2,1)}, bf16[2,2,128,384]{3,2,1,0:T(8,128)(2,1)}, u32[]{:S(2)}, u32[]{:S(2)}) collective-permute-start(bf16[2,2,128,384]{3,2,1,0:T(8,128)(2,1)} %get-tuple-element.120.refs_4_), channel_id=1, source_target_pairs={{0,4},{1,5},{2,6},{3,7},{4,0},{5,1},{6,2},{7,3},{8,12},{9,13},{10,... | collective-permute-start | bytes 1179656 | tf_op jit(solution)/shard_map/ppermute | solution.py:528
  249.0 12.2 %collective-permute-start.11 = (bf16[2,2,128,384]{3,2,1,0:T(8,128)(2,1)}, bf16[2,2,128,384]{3,2,1,0:T(8,128)(2,1)}, u32[]{:S(2)}, u32[]{:S(2)}) collective-permute-start(bf16[2,2,128,384]{3,2,1,0:T(8,128)(2,1)} %get-tuple-element.121.refs_8_), channel_id=1, source_target_pairs={{0,8},{1,9},{2,10},{3,11},{4,12},{5,13},{6,14},{7,15},{8,0},{9,1},... | collective-permute-start | bytes 1179656 | tf_op jit(solution)/shard_map/ppermute | solution.py:528
  249.8 25.7 %collective-permute-start.9 = (bf16[2,2,128,384]{3,2,1,0:T(8,128)(2,1)}, bf16[2,2,128,384]{3,2,1,0:T(8,128)(2,1)}, u32[]{:S(2)}, u32[]{:S(2)}) collective-permute-start(bf16[2,2,128,384]{3,2,1,0:T(8,128)(2,1)} %get-tuple-element.119.refs_0_), channel_id=1, source_target_pairs={{0,2},{1,3},{2,0},{3,1},{4,6},{5,7},{6,4},{7,5},{8,10},{9,11},{10,... | collective-permute-start | bytes 1179656 | tf_op jit(solution)/shard_map/ppermute | solution.py:528
  251.0 40.7 %collective-permute-start.4 = (bf16[4,2,128,384]{3,2,1,0:T(8,128)(2,1)}, bf16[4,2,128,384]{3,2,1,0:T(8,128)(2,1)}, u32[]{:S(2)}, u32[]{:S(2)}) collective-permute-start(bf16[4,2,128,384]{3,2,1,0:T(8,128)(2,1)} %get-tuple-element.110.refs_4_), channel_id=1, source_target_pairs={{0,4},{1,5},{2,6},{3,7},{4,0},{5,1},{6,2},{7,3},{8,12},{9,13},{10,... | collective-permute-start | bytes 2359304 | tf_op jit(solution)/shard_map/ppermute | solution.py:528
  260.0 32.5 %collective-permute-start.5 = (bf16[4,2,128,384]{3,2,1,0:T(8,128)(2,1)}, bf16[4,2,128,384]{3,2,1,0:T(8,128)(2,1)}, u32[]{:S(2)}, u32[]{:S(2)}) collective-permute-start(bf16[4,2,128,384]{3,2,1,0:T(8,128)(2,1)} %get-tuple-element.111.refs_8_), channel_id=1, source_target_pairs={{0,8},{1,9},{2,10},{3,11},{4,12},{5,13},{6,14},{7,15},{8,0},{9,1},... | collective-permute-start | bytes 2359304 | tf_op jit(solution)/shard_map/ppermute | solution.py:528
  275.5 18.4 %collective-permute-start.12 = (bf16[2,2,128,384]{3,2,1,0:T(8,128)(2,1)}, bf16[2,2,128,384]{3,2,1,0:T(8,128)(2,1)}, u32[]{:S(2)}, u32[]{:S(2)}) collective-permute-start(bf16[2,2,128,384]{3,2,1,0:T(8,128)(2,1)} %collective-permute-done.9.refs_1_), channel_id=1, source_target_pairs={{0,1},{1,0},{2,3},{3,2},{4,5},{5,4},{6,7},{7,6},{8,9},{9,8},{10,11... | collective-permute-start | bytes 1179656 | tf_op jit(solution)/shard_map/ppermute | solution.py:528
  275.5 18.4 %collective-permute-start.13 = (bf16[2,2,128,384]{3,2,1,0:T(8,128)(2,1)}, bf16[2,2,128,384]{3,2,1,0:T(8,128)(2,1)}, u32[]{:S(2)}, u32[]{:S(2)}) collective-permute-start(bf16[2,2,128,384]{3,2,1,0:T(8,128)(2,1)} %collective-permute-done.10.refs_5_), channel_id=1, source_target_pairs={{0,1},{1,0},{2,3},{3,2},{4,5},{5,4},{6,7},{7,6},{8,9},{9,8},{10,11... | collective-permute-start | bytes 1179656 | tf_op jit(solution)/shard_map/ppermute | solution.py:528
  276.0 18.4 %collective-permute-start.14 = (bf16[2,2,128,384]{3,2,1,0:T(8,128)(2,1)}, bf16[2,2,128,384]{3,2,1,0:T(8,128)(2,1)}, u32[]{:S(2)}, u32[]{:S(2)}) collective-permute-start(bf16[2,2,128,384]{3,2,1,0:T(8,128)(2,1)} %collective-permute-done.11.refs_9_), channel_id=1, source_target_pairs={{0,1},{1,0},{2,3},{3,2},{4,5},{5,4},{6,7},{7,6},{8,9},{9,8},{10,11... | collective-permute-start | bytes 1179656 | tf_op jit(solution)/shard_map/ppermute | solution.py:528
  291.7 50.9 %collective-permute-start = (bf16[9,2,128,384]{3,2,1,0:T(8,128)(2,1)}, bf16[9,2,128,384]{3,2,1,0:T(8,128)(2,1)}, u32[]{:S(2)}, u32[]{:S(2)}) collective-permute-start(bf16[9,2,128,384]{3,2,1,0:T(8,128)(2,1)} %get-tuple-element.106.refs_0_), channel_id=1, source_target_pairs={{0,2},{1,3},{2,0},{3,1},{4,6},{5,7},{6,4},{7,5},{8,10},{9,11},{10,... | collective-permute-start | bytes 5308424 | tf_op jit(solution)/shard_map/ppermute | solution.py:528
  292.5 50.1 %collective-permute-start.1 = (bf16[9,2,128,384]{3,2,1,0:T(8,128)(2,1)}, bf16[9,2,128,384]{3,2,1,0:T(8,128)(2,1)}, u32[]{:S(2)}, u32[]{:S(2)}) collective-permute-start(bf16[9,2,128,384]{3,2,1,0:T(8,128)(2,1)} %get-tuple-element.107.refs_4_), channel_id=1, source_target_pairs={{0,4},{1,5},{2,6},{3,7},{4,0},{5,1},{6,2},{7,3},{8,12},{9,13},{10,... | collective-permute-start | bytes 5308424 | tf_op jit(solution)/shard_map/ppermute | solution.py:528
  293.9 17.2 %collective-permute-start.6 = (bf16[4,2,128,384]{3,2,1,0:T(8,128)(2,1)}, bf16[4,2,128,384]{3,2,1,0:T(8,128)(2,1)}, u32[]{:S(2)}, u32[]{:S(2)}) collective-permute-start(bf16[4,2,128,384]{3,2,1,0:T(8,128)(2,1)} %collective-permute-done.3.refs_1_), channel_id=1, source_target_pairs={{0,1},{1,0},{2,3},{3,2},{4,5},{5,4},{6,7},{7,6},{8,9},{9,8},{10,11... | collective-permute-start | bytes 2359304 | tf_op jit(solution)/shard_map/ppermute | solution.py:528
  293.9 18.0 %collective-permute-start.7 = (bf16[4,2,128,384]{3,2,1,0:T(8,128)(2,1)}, bf16[4,2,128,384]{3,2,1,0:T(8,128)(2,1)}, u32[]{:S(2)}, u32[]{:S(2)}) collective-permute-start(bf16[4,2,128,384]{3,2,1,0:T(8,128)(2,1)} %collective-permute-done.4.refs_5_), channel_id=1, source_target_pairs={{0,1},{1,0},{2,3},{3,2},{4,5},{5,4},{6,7},{7,6},{8,9},{9,8},{10,11... | collective-permute-start | bytes 2359304 | tf_op jit(solution)/shard_map/ppermute | solution.py:528
  294.4 17.5 %collective-permute-start.8 = (bf16[4,2,128,384]{3,2,1,0:T(8,128)(2,1)}, bf16[4,2,128,384]{3,2,1,0:T(8,128)(2,1)}, u32[]{:S(2)}, u32[]{:S(2)}) collective-permute-start(bf16[4,2,128,384]{3,2,1,0:T(8,128)(2,1)} %collective-permute-done.5.refs_9_), channel_id=1, source_target_pairs={{0,1},{1,0},{2,3},{3,2},{4,5},{5,4},{6,7},{7,6},{8,9},{9,8},{10,11... | collective-permute-start | bytes 2359304 | tf_op jit(solution)/shard_map/ppermute | solution.py:528
  311.1 41.3 %collective-permute-start.2 = (bf16[9,2,128,384]{3,2,1,0:T(8,128)(2,1)}, bf16[9,2,128,384]{3,2,1,0:T(8,128)(2,1)}, u32[]{:S(2)}, u32[]{:S(2)}) collective-permute-start(bf16[9,2,128,384]{3,2,1,0:T(8,128)(2,1)} %get-tuple-element.108.refs_8_), channel_id=1, source_target_pairs={{0,8},{1,9},{2,10},{3,11},{4,12},{5,13},{6,14},{7,15},{8,0},{9,1},... | collective-permute-start | bytes 5308424 | tf_op jit(solution)/shard_map/ppermute | solution.py:528
  352.4 4.0 collective-permute-start.15
  352.4 6.6 %collective-permute-start.16 = (bf16[9,2,128,384]{3,2,1,0:T(8,128)(2,1)}, bf16[9,2,128,384]{3,2,1,0:T(8,128)(2,1)}, u32[]{:S(2)}, u32[]{:S(2)}) collective-permute-start(bf16[9,2,128,384]{3,2,1,0:T(8,128)(2,1)} %collective-permute-done.1.refs_5_), channel_id=1, source_target_pairs={{0,1},{1,0},{2,3},{3,2},{4,5},{5,4},{6,7},{7,6},{8,9},{9,8},{10,11... | collective-permute-start | bytes 5308424 | tf_op jit(solution)/shard_map/ppermute | solution.py:528
  352.9 8.6 %collective-permute-start.17 = (bf16[9,2,128,384]{3,2,1,0:T(8,128)(2,1)}, bf16[9,2,128,384]{3,2,1,0:T(8,128)(2,1)}, u32[]{:S(2)}, u32[]{:S(2)}) collective-permute-start(bf16[9,2,128,384]{3,2,1,0:T(8,128)(2,1)} %collective-permute-done.2.refs_9_), channel_id=1, source_target_pairs={{0,1},{1,0},{2,3},{3,2},{4,5},{5,4},{6,7},{7,6},{8,9},{9,8},{10,11... | collective-permute-start | bytes 5308424 | tf_op jit(solution)/shard_map/ppermute | solution.py:528
